TPU v7x, 32 devices: a whole 2x2x4 slice. The times are simulated.
32 devices in a mesh: col: 8 (over z, y), row: 4 (over x, core).
Axes of the slice: x: 2, y: 2, z: 4, core: 2. Of those that a mesh axis runs over, the one named last changes fastest.
Arguments:
- right_side: float32 [8192, 256], P(('row', 'col')), may hold values from -6 to 6
- prior_solution: bfloat16 [16384, 256], P('col'), may hold values from -6 to 6
- factor_codes: bfloat16 [8192, 16384], P('row', 'col'), may hold values from -0.046875 to 0.046875
- block_scale: float32 [4, 64], P('row', 'col'), may hold values from 0.3 to 3
- diag_inverse: bfloat16 [4, 2048, 2048], P('row', 'col'), may hold values from -0.125 to 0.125
- inner_factor: bfloat16 [4, 4, 2048, 2048], P('row', None, 'col'), may hold values from -0.125 to 0.125
Outputs:
- solved: float32 [8192, 256], P(('row', 'col'))
All inputs are finite; a program needn't handle non-finite values.
Results may differ from a plain program's by a relative error of at most 0.0095.
Values may be sent and summed in bfloat16 or wider, within the bound.
No kernel may reach another device: no remote copies, remote signals or barrier semaphores. Data moves between devices by JAX's collectives and lax.ppermute only.
A program may use at most 64 MiB of HBM per device.

v0:
```python
import jax
import jax.numpy as jnp
from jax import lax
from jax.sharding import PartitionSpec as P


def from_root(value, axis, source):
    kept = jnp.where(lax.axis_index(axis) == source, value, 0).astype(value.dtype)
    return lax.psum(kept, axis)


def local(right_side, prior_solution, factor_codes, block_scale, diag_inverse, inner_factor):
    rows_each = right_side.shape[0]
    panel_rows = factor_codes.shape[0]
    blocks_here = block_scale.shape[1]
    block_cols = factor_codes.shape[1] // blocks_here
    columns_out = right_side.shape[1]
    summed = jnp.zeros((panel_rows, columns_out), jnp.float32)
    for column_block in range(blocks_here):
        coded = lax.dynamic_slice(
            factor_codes, (0, column_block * block_cols), (panel_rows, block_cols)
        )
        earlier = prior_solution[column_block * block_cols : (column_block + 1) * block_cols]
        summed = summed + block_scale[0, column_block] * jnp.dot(
            coded, earlier, preferred_element_type=jnp.float32
        )
    prior_rows = lax.psum_scatter(summed, "col", scatter_dimension=0, tiled=True)
    rhs = right_side - prior_rows
    row_place = lax.axis_index("row")
    solved = jnp.zeros((rows_each, columns_out), jnp.float32)
    inverse_rows = diag_inverse[0]
    panel_count = lax.axis_size("row")
    for section in range(panel_count):
        rounded = rhs.astype(jnp.bfloat16)
        current = jnp.dot(
            inverse_rows,
            lax.all_gather(rounded, "col", axis=0, tiled=True),
            preferred_element_type=jnp.float32,
        )
        solved = jnp.where(row_place == section, current, solved)
        if section + 1 < panel_count:
            sending = current.astype(jnp.bfloat16)
            coupling = inner_factor[0, section]
            whole_panel = lax.all_gather(sending, "col", axis=0, tiled=True)
            copied = from_root(whole_panel, "row", section)
            update = jnp.dot(coupling, copied, preferred_element_type=jnp.float32)
            rhs = rhs - jnp.where(row_place > section, update, 0.0)
    return solved


def solution(mesh):
    return jax.shard_map(
        local,
        mesh=mesh,
        in_specs=(
            P(("row", "col"), None),
            P("col", None),
            P("row", "col"),
            P("row", "col"),
            P("row", "col", None),
            P("row", None, "col", None),
        ),
        out_specs=P(("row", "col"), None),
        check_vma=False,
    )
```

profile of v0, /device:TPU:0, one launch (start us, length us, event | category | flops | bytes accessed | tf_op | source)
XLA Modules:
  0.0 509.4 jit_solution(15707440207164434849)
XLA Ops:
  6.5 1.6 fusion.45
  8.2 2.5 convolution_multiply_fusion.7
  10.7 2.5 fusion.6
  13.3 2.0 fusion.5
  15.3 1.1 fusion.4
  16.4 1.1 fusion.3
  17.5 1.1 fusion.2
  18.6 1.0 fusion.1
  19.6 2.4 fusion
  22.1 71.2 %reduce-scatter.2.cloned.1.call-done = f32[256,256]{1,0:T(8,128)} async-done(((f32[2048,256]{1,0:T(8,128)}), f32[256,256]{1,0:T(8,128)}) %reduce-scatter.2.cloned.1.call-update) | async-done | bytes 262160 | tf_op jit(solution)/shard_map/reduce_scatter | solution.py:27
  93.2 1.6 fusion.44
  95.0 39.7 %all-gather.8.cloned.1.call-done = bf16[2048,256]{1,0:T(8,128)(2,1)} async-done(((bf16[256,256]{1,0:T(8,128)(2,1)}), bf16[2048,256]{1,0:T(8,128)(2,1)}) %all-gather.8.cloned.1.call-update) | async-done | bytes 1048592 | tf_op jit(solution)/shard_map/all_gather | solution.py:37
  134.7 1.7 fusion.23
  136.4 0.7 convert_bitcast_fusion.2
  137.2 38.2 %all-gather.10.cloned.1.call-done = bf16[2048,256]{0,1:T(8,128)(2,1)} async-done(((bf16[256,256]{0,1:T(8,128)(2,1)}), bf16[2048,256]{0,1:T(8,128)(2,1)}) %all-gather.10.cloned.1.call-update) | async-done | bytes 1048592 | tf_op jit(solution)/shard_map/all_gather | solution.py:44
  175.4 2.3 broadcast_select_fusion.2
  177.7 35.2 %all-reduce.4.cloned.1.call-done = bf16[2048,256]{0,1:T(8,128)(2,1)} async-done(((bf16[2048,256]{0,1:T(8,128)(2,1)}), bf16[2048,256]{0,1:T(8,128)(2,1)}) %all-reduce.4.cloned.1.call-update) | async-done | bytes 1048592 | tf_op jit(solution)/shard_map/psum | solution.py:9
  212.9 2.7 fusion.46
  215.7 40.9 %all-gather.12.cloned.1.call-done = bf16[2048,256]{1,0:T(8,128)(2,1)} async-done(((bf16[256,256]{1,0:T(8,128)(2,1)}), bf16[2048,256]{1,0:T(8,128)(2,1)}) %all-gather.12.cloned.1.call-update) | async-done | bytes 1048592 | tf_op jit(solution)/shard_map/all_gather | solution.py:37
  256.5 1.7 fusion.21
  259.0 38.2 %all-gather.14.cloned.1.call-done = bf16[2048,256]{0,1:T(8,128)(2,1)} async-done(((bf16[256,256]{0,1:T(8,128)(2,1)}), bf16[2048,256]{0,1:T(8,128)(2,1)}) %all-gather.14.cloned.1.call-update) | async-done | bytes 1048592 | tf_op jit(solution)/shard_map/all_gather | solution.py:44
  297.2 1.1 broadcast_select_fusion.1
  298.3 36.5 %all-reduce.6.cloned.1.call-done = bf16[2048,256]{0,1:T(8,128)(2,1)} async-done(((bf16[2048,256]{0,1:T(8,128)(2,1)}), bf16[2048,256]{0,1:T(8,128)(2,1)}) %all-reduce.6.cloned.1.call-update) | async-done | bytes 1048592 | tf_op jit(solution)/shard_map/psum | solution.py:9
  334.9 2.7 fusion.47
  337.6 40.9 %all-gather.16.cloned.1.call-done = bf16[2048,256]{1,0:T(8,128)(2,1)} async-done(((bf16[256,256]{1,0:T(8,128)(2,1)}), bf16[2048,256]{1,0:T(8,128)(2,1)}) %all-gather.16.cloned.1.call-update) | async-done | bytes 1048592 | tf_op jit(solution)/shard_map/all_gather | solution.py:37
  378.5 1.7 fusion.19
  381.0 38.2 %all-gather.18.cloned.1.call-done = bf16[2048,256]{0,1:T(8,128)(2,1)} async-done(((bf16[256,256]{0,1:T(8,128)(2,1)}), bf16[2048,256]{0,1:T(8,128)(2,1)}) %all-gather.18.cloned.1.call-update) | async-done | bytes 1048592 | tf_op jit(solution)/shard_map/all_gather | solution.py:44
  419.2 1.1 broadcast_select_fusion
  420.3 36.6 %all-reduce.8.cloned.1.call-done = bf16[2048,256]{0,1:T(8,128)(2,1)} async-done(((bf16[2048,256]{0,1:T(8,128)(2,1)}), bf16[2048,256]{0,1:T(8,128)(2,1)}) %all-reduce.8.cloned.1.call-update) | async-done | bytes 1048592 | tf_op jit(solution)/shard_map/psum | solution.py:9
  456.9 2.7 fusion.14
  460.0 40.5 %all-gather.20.cloned.1.call-done = bf16[2048,256]{1,0:T(8,128)(2,1)} async-done(((bf16[256,256]{1,0:T(8,128)(2,1)}), bf16[2048,256]{1,0:T(8,128)(2,1)}) %all-gather.20.cloned.1.call-update) | async-done | bytes 1048592 | tf_op jit(solution)/shard_map/all_gather | solution.py:37
  500.5 2.4 fusion.7
  (35 shorter events, 2.3 us)
Async XLA Ops:
  6.5 128.2 %copy-start = (bf16[1,256,2048]{2,1,0:T(8,128)(2,1)S(1)}, bf16[1,256,2048]{2,1,0:T(8,128)(2,1)}, u32[]{:S(2)}) copy-start(bf16[1,256,2048]{2,1,0:T(8,128)(2,1)} %param.10) | copy-start | bytes 3145732
  6.5 86.7 %reduce-scatter.2.cloned.1.call-start = ((), (), s32[]{:S(2)}) async-start(), calls=%async_computation.1 | async-start | bytes 2359296 | tf_op jit(solution)/shard_map/reduce_scatter | solution.py:27
  8.2 5.1 copy-start.1
  13.3 2.0 copy-start.2
  22.0 71.2 %copy-start.3 = (f32[256,256]{1,0:T(8,128)S(1)}, f32[256,256]{1,0:T(8,128)}, u32[]{:S(2)}) copy-start(f32[256,256]{1,0:T(8,128)} %param.6) | copy-start | bytes 786436
  22.0 112.7 %all-gather.8.cloned.1.call-start = ((), (), s32[]{:S(2)}) async-start(), calls=%async_computation.2 | async-start | bytes 1179648 | tf_op jit(solution)/shard_map/all_gather | solution.py:37
  94.9 80.5 %all-gather.10.cloned.1.call-start = ((), (), s32[]{:S(2)}) async-start(), calls=%async_computation.3 | async-start | bytes 1179648 | tf_op jit(solution)/shard_map/all_gather | solution.py:44
  137.1 75.8 %all-reduce.4.cloned.1.call-start = ((), (), s32[]{:S(2)}) async-start(), calls=%async_computation.4 | async-start | bytes 2097152 | tf_op jit(solution)/shard_map/psum | solution.py:9
  177.7 78.9 %all-gather.12.cloned.1.call-start = ((), (), s32[]{:S(2)}) async-start(), calls=%async_computation.5 | async-start | bytes 1179648 | tf_op jit(solution)/shard_map/all_gather | solution.py:37
  215.6 81.6 %all-gather.14.cloned.1.call-start = ((), (), s32[]{:S(2)}) async-start(), calls=%async_computation.6 | async-start | bytes 1179648 | tf_op jit(solution)/shard_map/all_gather | solution.py:44
  258.9 75.9 %all-reduce.6.cloned.1.call-start = ((), (), s32[]{:S(2)}) async-start(), calls=%async_computation.7 | async-start | bytes 2097152 | tf_op jit(solution)/shard_map/psum | solution.py:9
  298.3 80.2 %all-gather.16.cloned.1.call-start = ((), (), s32[]{:S(2)}) async-start(), calls=%async_computation.8 | async-start | bytes 1179648 | tf_op jit(solution)/shard_map/all_gather | solution.py:37
  337.6 81.6 %all-gather.18.cloned.1.call-start = ((), (), s32[]{:S(2)}) async-start(), calls=%async_computation.9 | async-start | bytes 1179648 | tf_op jit(solution)/shard_map/all_gather | solution.py:44
  380.9 76.0 %all-reduce.8.cloned.1.call-start = ((), (), s32[]{:S(2)}) async-start(), calls=%async_computation.10 | async-start | bytes 2097152 | tf_op jit(solution)/shard_map/psum | solution.py:9
  420.2 80.3 %all-gather.20.cloned.1.call-start = ((), (), s32[]{:S(2)}) async-start(), calls=%async_computation.11 | async-start | bytes 1179648 | tf_op jit(solution)/shard_map/all_gather | solution.py:37
Sparse Core Ops, SparseCore 0:
  22.2 71.0 reduce-scatter.1
  95.4 39.2 all-gather.7
  137.2 38.0 all-gather.9
  177.8 35.0 all-reduce.3
  215.8 40.7 all-gather.11
  259.1 38.0 all-gather.13
  299.6 35.2 all-reduce.5
  337.7 40.7 all-gather.15
  381.0 38.0 all-gather.17
  421.4 35.4 all-reduce.7
  459.7 40.7 all-gather.19
where the time goes:
time: 510 us; the launch traced here: 509 us
  waiting for transfers between devices  456 us (89%)
  matrix products  29.3 us (6%)
  between operations  13.4 us (3%)
  other arithmetic  8.06 us (2%)
    all_gather x4, waiting for transfers between devices, local(): lax.all_gather(rounded, 'col', axis=0, tiled=True)  162 us
    all_gather x3, waiting for transfers between devices, local(): whole_panel = lax.all_gather(sending, 'col', axis=0, tiled=True)  115 us
    psum x3, waiting for transfers between devices, from_root(): return lax.psum(kept, axis)  108 us
    reduce_scatter x1, waiting for transfers between devices, local(): lax.psum_scatter(summed, 'col', scatter_dimension=0, tiled=True)  71.2 us
    dot_general x8, matrix products, local(): jnp.dot(coded, earlier, preferred_element_type=jnp.float32)  13.7 us
  transfers between devices with their start and end apart: 11, of which 11 were waited for; matrix products, arithmetic and copies ran while one was open for 0% of the time, Pallas kernels for 0%

commit v1 on v0

--- a/solution.py
+++ b/solution.py
@@ -41,7 +41,9 @@
         if section + 1 < panel_count:
             sending = current.astype(jnp.bfloat16)
             coupling = inner_factor[0, section]
-            whole_panel = lax.all_gather(sending, "col", axis=0, tiled=True)
+            whole_panel = jnp.concatenate(
+                lax.all_to_all(jnp.stack([sending] * lax.axis_size("col")), "col", 0, 0), axis=0
+            )
             copied = from_root(whole_panel, "row", section)
             update = jnp.dot(coupling, copied, preferred_element_type=jnp.float32)
             rhs = rhs - jnp.where(row_place > section, update, 0.0)

time: 510 us -> 477 us (0.935)
  waiting for transfers between devices: 456 us -> 412 us
  starting transfers between devices: 0.42 us -> 11 us
    all_gather x3 -> x0, waiting for transfers between devices: 115 us -> none  [local(): whole_panel = lax.all_gather(sending, 'col', axis=0, tiled=True)]
    all_to_all x0 -> x3, waiting for transfers between devices: none -> 73.2 us  [local(): lax.all_to_all(jnp.stack([sending] * lax.axis_size('col')), 'col', 0, 0)]
    all_to_all x0 -> x3, starting transfers between devices: none -> 10.7 us  [local(): lax.all_to_all(jnp.stack([sending] * lax.axis_size('col')), 'col', 0, 0)]
where the time goes in v1:
time: 477 us; the launch traced here: 476 us
  waiting for transfers between devices  412 us (86%)
  matrix products  29.2 us (6%)
  between operations  13.7 us (3%)
  starting transfers between devices  11 us (2%)
  local copies, waits for them, and re-layouts  5.58 us (1%)
  other arithmetic  4.8 us (1%)
    all_gather x4, waiting for transfers between devices, local(): lax.all_gather(rounded, 'col', axis=0, tiled=True)  162 us
    psum x3, waiting for transfers between devices, from_root(): return lax.psum(kept, axis)  106 us
    all_to_all x3, waiting for transfers between devices, local(): lax.all_to_all(jnp.stack([sending] * lax.axis_size('col')), 'col', 0, 0)  73.2 us
    reduce_scatter x1, waiting for transfers between devices, local(): lax.psum_scatter(summed, 'col', scatter_dimension=0, tiled=True)  71.2 us
    dot_general x8, matrix products, local(): jnp.dot(coded, earlier, preferred_element_type=jnp.float32)  13.8 us
    all_to_all x3, starting transfers between devices, local(): lax.all_to_all(jnp.stack([sending] * lax.axis_size('col')), 'col', 0, 0)  10.7 us
  transfers between devices with their start and end apart: 11, of which 11 were waited for; matrix products, arithmetic and copies ran while one was open for 0% of the time, Pallas kernels for 0%

profile of v1, /device:TPU:0, one launch (start us, length us, event | category | flops | bytes accessed | tf_op | source)
XLA Modules:
  0.0 476.5 jit_solution(8811132779592236687)
XLA Ops:
  6.5 1.6 fusion.45
  8.2 2.6 convolution_multiply_fusion.7
  10.8 2.4 fusion.6
  13.2 2.1 fusion.5
  15.3 1.1 fusion.4
  16.5 1.1 fusion.3
  19.6 2.4 fusion
  22.1 71.2 %reduce-scatter.2.cloned.1.call-done = f32[256,256]{1,0:T(8,128)} async-done(((f32[2048,256]{1,0:T(8,128)}), f32[256,256]{1,0:T(8,128)}) %reduce-scatter.2.cloned.1.call-update) | async-done | bytes 262160 | tf_op jit(solution)/shard_map/reduce_scatter | solution.py:27
  93.3 1.6 fusion.44
  95.0 39.7 %all-gather.5.cloned.1.call-done = bf16[2048,256]{1,0:T(8,128)(2,1)} async-done(((bf16[256,256]{1,0:T(8,128)(2,1)}), bf16[2048,256]{1,0:T(8,128)(2,1)}) %all-gather.5.cloned.1.call-update) | async-done | bytes 1048592 | tf_op jit(solution)/shard_map/all_gather | solution.py:37
  134.7 1.7 fusion.23
  136.6 1.1 stack.6
  137.7 3.6 all-to-all-start
  141.3 24.4 %all-to-all-done = bf16[8,256,256]{2,1,0:T(8,128)(2,1)S(1)} async-done(((bf16[8,256,256]{2,1,0:T(8,128)(2,1)}), bf16[8,256,256]{2,1,0:T(8,128)(2,1)S(1)}, u32[]{:S(2)}, u32[]{:S(2)}) %all-to-all-start) | async-done | bytes 1048608 | tf_op jit(solution)/shard_map/all_to_all | solution.py:45
  166.8 35.2 %all-reduce.4.cloned.1.call-done = bf16[2048,256]{1,0:T(8,128)(2,1)} async-done(((bf16[2048,256]{1,0:T(8,128)(2,1)}), bf16[2048,256]{1,0:T(8,128)(2,1)}) %all-reduce.4.cloned.1.call-update) | async-done | bytes 1048592 | tf_op jit(solution)/shard_map/psum | solution.py:9
  202.0 2.6 fusion.46
  204.7 40.9 %all-gather.7.cloned.1.call-done = bf16[2048,256]{1,0:T(8,128)(2,1)} async-done(((bf16[256,256]{1,0:T(8,128)(2,1)}), bf16[2048,256]{1,0:T(8,128)(2,1)}) %all-gather.7.cloned.1.call-update) | async-done | bytes 1048592 | tf_op jit(solution)/shard_map/all_gather | solution.py:37
  245.6 1.7 fusion.21
  247.4 1.1 stack.7
  248.5 3.6 all-to-all-start.1
  252.1 24.4 %all-to-all-done.1 = bf16[8,256,256]{2,1,0:T(8,128)(2,1)S(1)} async-done(((bf16[8,256,256]{2,1,0:T(8,128)(2,1)}), bf16[8,256,256]{2,1,0:T(8,128)(2,1)S(1)}, u32[]{:S(2)}, u32[]{:S(2)}) %all-to-all-start.1) | async-done | bytes 1048608 | tf_op jit(solution)/shard_map/all_to_all | solution.py:45
  277.6 35.2 %all-reduce.6.cloned.1.call-done = bf16[2048,256]{1,0:T(8,128)(2,1)} async-done(((bf16[2048,256]{1,0:T(8,128)(2,1)}), bf16[2048,256]{1,0:T(8,128)(2,1)}) %all-reduce.6.cloned.1.call-update) | async-done | bytes 1048592 | tf_op jit(solution)/shard_map/psum | solution.py:9
  312.9 2.6 fusion.47
  315.5 40.9 %all-gather.9.cloned.1.call-done = bf16[2048,256]{1,0:T(8,128)(2,1)} async-done(((bf16[256,256]{1,0:T(8,128)(2,1)}), bf16[2048,256]{1,0:T(8,128)(2,1)}) %all-gather.9.cloned.1.call-update) | async-done | bytes 1048592 | tf_op jit(solution)/shard_map/all_gather | solution.py:37
  356.4 1.7 fusion.19
  358.3 1.1 stack.8
  359.4 3.6 all-to-all-start.2
  363.0 24.4 %all-to-all-done.2 = bf16[8,256,256]{2,1,0:T(8,128)(2,1)S(1)} async-done(((bf16[8,256,256]{2,1,0:T(8,128)(2,1)}), bf16[8,256,256]{2,1,0:T(8,128)(2,1)S(1)}, u32[]{:S(2)}, u32[]{:S(2)}) %all-to-all-start.2) | async-done | bytes 1048608 | tf_op jit(solution)/shard_map/all_to_all | solution.py:45
  388.5 35.2 %all-reduce.8.cloned.1.call-done = bf16[2048,256]{1,0:T(8,128)(2,1)} async-done(((bf16[2048,256]{1,0:T(8,128)(2,1)}), bf16[2048,256]{1,0:T(8,128)(2,1)}) %all-reduce.8.cloned.1.call-update) | async-done | bytes 1048592 | tf_op jit(solution)/shard_map/psum | solution.py:9
  423.7 2.6 fusion.14
  426.8 40.5 %all-gather.11.cloned.1.call-done = bf16[2048,256]{1,0:T(8,128)(2,1)} async-done(((bf16[256,256]{1,0:T(8,128)(2,1)}), bf16[2048,256]{1,0:T(8,128)(2,1)}) %all-gather.11.cloned.1.call-update) | async-done | bytes 1048592 | tf_op jit(solution)/shard_map/all_gather | solution.py:37
  467.3 2.4 fusion.7
  (38 shorter events, 6.3 us)
Async XLA Ops:
  6.5 128.2 %copy-start = (bf16[1,256,2048]{2,1,0:T(8,128)(2,1)S(1)}, bf16[1,256,2048]{2,1,0:T(8,128)(2,1)}, u32[]{:S(2)}) copy-start(bf16[1,256,2048]{2,1,0:T(8,128)(2,1)} %param.10) | copy-start | bytes 3145732
  6.5 86.8 %reduce-scatter.2.cloned.1.call-start = ((), (), s32[]{:S(2)}) async-start(), calls=%async_computation.4 | async-start | bytes 2359296 | tf_op jit(solution)/shard_map/reduce_scatter | solution.py:27
  8.2 5.1 %copy-start.1 = (bf16[2048,2048]{1,0:T(8,128)(2,1)S(1)}, bf16[2048,2048]{1,0:T(8,128)(2,1)}, u32[]{:S(2)}) copy-start(bf16[2048,2048]{1,0:T(8,128)(2,1)} %param.8) | copy-start | bytes 25165828
  13.2 2.1 copy-start.2
  22.0 71.3 %copy-start.3 = (f32[256,256]{1,0:T(8,128)S(1)}, f32[256,256]{1,0:T(8,128)}, u32[]{:S(2)}) copy-start(f32[256,256]{1,0:T(8,128)} %param.6) | copy-start | bytes 786436
  22.1 112.7 %all-gather.5.cloned.1.call-start = ((), (), s32[]{:S(2)}) async-start(), calls=%async_computation.5 | async-start | bytes 1179648 | tf_op jit(solution)/shard_map/all_gather | solution.py:37
  137.7 28.0 %all-to-all-start = ((bf16[8,256,256]{2,1,0:T(8,128)(2,1)}), bf16[8,256,256]{2,1,0:T(8,128)(2,1)S(1)}, u32[]{:S(2)}, u32[]{:S(2)}) async-start(bf16[8,256,256]{2,1,0:T(8,128)(2,1)} %stack.6), calls=%async_computation.1 | async-start | bytes 2097152 | tf_op jit(solution)/shard_map/all_to_all | solution.py:45
  141.2 60.8 %all-reduce.4.cloned.1.call-start = ((), (), s32[]{:S(2)}) async-start(), calls=%async_computation.6 | async-start | bytes 2097152 | tf_op jit(solution)/shard_map/psum | solution.py:9
  166.7 78.8 %all-gather.7.cloned.1.call-start = ((), (), s32[]{:S(2)}) async-start(), calls=%async_computation.7 | async-start | bytes 1179648 | tf_op jit(solution)/shard_map/all_gather | solution.py:37
  248.5 28.0 %all-to-all-start.1 = ((bf16[8,256,256]{2,1,0:T(8,128)(2,1)}), bf16[8,256,256]{2,1,0:T(8,128)(2,1)S(1)}, u32[]{:S(2)}, u32[]{:S(2)}) async-start(bf16[8,256,256]{2,1,0:T(8,128)(2,1)} %stack.7), calls=%async_computation.2 | async-start | bytes 2097152 | tf_op jit(solution)/shard_map/all_to_all | solution.py:45
  252.1 60.8 %all-reduce.6.cloned.1.call-start = ((), (), s32[]{:S(2)}) async-start(), calls=%async_computation.8 | async-start | bytes 2097152 | tf_op jit(solution)/shard_map/psum | solution.py:9
  277.6 78.8 %all-gather.9.cloned.1.call-start = ((), (), s32[]{:S(2)}) async-start(), calls=%async_computation.9 | async-start | bytes 1179648 | tf_op jit(solution)/shard_map/all_gather | solution.py:37
  359.4 28.0 %all-to-all-start.2 = ((bf16[8,256,256]{2,1,0:T(8,128)(2,1)}), bf16[8,256,256]{2,1,0:T(8,128)(2,1)S(1)}, u32[]{:S(2)}, u32[]{:S(2)}) async-start(bf16[8,256,256]{2,1,0:T(8,128)(2,1)} %stack.8), calls=%async_computation.3 | async-start | bytes 2097152 | tf_op jit(solution)/shard_map/all_to_all | solution.py:45
  362.9 60.8 %all-reduce.8.cloned.1.call-start = ((), (), s32[]{:S(2)}) async-start(), calls=%async_computation.10 | async-start | bytes 2097152 | tf_op jit(solution)/shard_map/psum | solution.py:9
  388.4 78.8 %all-gather.11.cloned.1.call-start = ((), (), s32[]{:S(2)}) async-start(), calls=%async_computation.11 | async-start | bytes 1179648 | tf_op jit(solution)/shard_map/all_gather | solution.py:37
Sparse Core Ops, SparseCore 0:
  22.2 71.0 reduce-scatter.1
  95.4 39.2 all-gather.4
  166.9 35.1 all-reduce.3
  204.8 40.7 all-gather.6
  277.7 35.1 all-reduce.5
  315.6 40.7 all-gather.8
  388.6 35.1 all-reduce.7
  426.5 40.7 all-gather.10
